TPU v7x, 32 devices: a whole 2x2x4 slice. The times are simulated.
32 devices in a mesh: north: 4 (over x, core), east: 8 (over z, y).
Axes of the slice: x: 2, y: 2, z: 4, core: 2. Of those that a mesh axis runs over, the one named last changes fastest.
Arguments:
- left_factor: bfloat16 [4096, 2048], P('north', 'east'), may hold values from -6 to 6
- right_factor: bfloat16 [2048, 4096], P('north', 'east'), may hold values from -0.125 to 0.125
Outputs:
- updated: float32 [4096, 4096], P('north', 'east')
All inputs are finite; a program needn't handle non-finite values.
Results may differ from a plain program's by a relative error of at most 0.0003.
Values may be sent and summed in bfloat16 or wider, within the bound.
A program may use at most 128 MiB of HBM per device.

v0:
```python
import jax
import jax.numpy as jnp
from jax import lax
from jax.sharding import PartitionSpec as P


def over_all(piece, axis, dim, lap, start):

    def gathered(part):
        return lax.all_gather(part, axis, axis=dim, tiled=True)

    return lap(start, jax.tree.map(gathered, piece), jnp.int32(0))


def absorb_panel(carry, left_panel, right_panel):
    return carry + jnp.dot(left_panel, right_panel, preferred_element_type=jnp.float32)


def shards(left_factor, right_factor):
    begin = jnp.zeros((left_factor.shape[0], right_factor.shape[1]), jnp.float32)
    left_line = lax.all_gather(left_factor, "east", axis=1, tiled=True)

    def take_rows(carry, piece, start):
        left_piece = lax.dynamic_slice_in_dim(left_line, start, piece.shape[0], axis=1)
        return absorb_panel(carry, left_piece, piece)

    total = over_all(right_factor, "north", 0, take_rows, begin)
    updated = total
    row_power = lax.psum(jnp.sum(updated * updated, axis=1), "east")
    updated = (
        updated * lax.rsqrt(row_power / (updated.shape[1] * lax.axis_size("east")) + 1e-06)[:, None]
    )
    return updated


def solution(mesh):
    placed = (P("north", "east"), P("north", "east"))
    return jax.shard_map(
        shards, mesh=mesh, in_specs=placed, out_specs=P("north", "east"), check_vma=False
    )
```

profile of v0, /device:TPU:0, one launch (start us, length us, event | category | flops | bytes accessed | tf_op | source)
XLA Modules:
  0.0 146.5 jit_solution(11622587532451686640)
XLA Ops:
  6.5 0.0 all-gather.5.cloned.1.call-start
  6.5 0.7 all-gather.5.cloned.1.call-update
  7.3 0.0 all-gather.3.cloned.1.call-start
  7.3 0.7 all-gather.3.cloned.1.call-update
  8.0 26.2 %all-gather.5.cloned.1.call-done = bf16[2048,512]{1,0:T(8,128)(2,1)} async-done(((bf16[512,512]{1,0:T(8,128)(2,1)}), bf16[2048,512]{1,0:T(8,128)(2,1)}) %all-gather.5.cloned.1.call-update) | async-done | bytes 2097168 | tf_op jit(solution)/shard_map/all_gather | solution.py:10
  34.2 76.7 %all-gather.3.cloned.1.call-done = bf16[1024,2048]{1,0:T(8,128)(2,1)} async-done(((bf16[1024,256]{1,0:T(8,128)(2,1)}), bf16[1024,2048]{1,0:T(8,128)(2,1)}) %all-gather.3.cloned.1.call-update) | async-done | bytes 4194320 | tf_op jit(solution)/shard_map/all_gather | solution.py:21
  110.9 6.6 %multiply_reduce_fusion = (f32[1024]{0:T(1024)S(1)}, f32[1024,512]{0,1:T(8,128)}) fusion(bf16[1024,2048]{1,0:T(8,128)(2,1)} %all-gather.3.cloned.1.call-done, bf16[2048,512]{1,0:T(8,128)(2,1)} %all-gather.5.cloned.1.call-done), kind=kOutput, calls=%fused_computation | convolution fusion | flops 2148531200 | bytes 8392704 | tf_op jit(solution)/shard_map/dot_general | solution.py:16
  117.5 18.6 %psum.7 = f32[1024]{0:T(1024)S(1)} all-reduce(f32[1024]{0:T(1024)S(1)} %get-tuple-element.5), channel_id=1, replica_groups=mesh['north'=4,'east'=8] {'east'}, use_global_device_ids=true, to_apply=%region_1.0 | all-reduce | flops 1024 | bytes 8192 | tf_op jit(solution)/shard_map/psum | solution.py:29
  136.0 1.8 %broadcast_multiply_fusion = f32[1024,512]{0,1:T(8,128)S(1)} fusion(f32[1024,512]{0,1:T(8,128)} %get-tuple-element.6, f32[1024]{0:T(1024)S(1)} %add_rsqrt_fusion), kind=kLoop, calls=%fused_computation.1 | loop fusion | flops 524288 | bytes 4198400 | tf_op jit(solution)/shard_map/mul | solution.py:31
  137.9 1.8 %copy.3 = f32[1024,512]{1,0:T(8,128)} copy(f32[1024,512]{0,1:T(8,128)S(1)} %broadcast_multiply_fusion) | data formatting | bytes 4194304 | tf_op jit(solution)/shard_map/mul | solution.py:31
  (1 shorter events, 0.0 us)
Async XLA Ops:
  6.5 27.7 %all-gather.5.cloned.1.call-start = ((), (), s32[]{:S(2)}) async-start(), calls=%async_computation.1 | async-start | bytes 2621440 | tf_op jit(solution)/shard_map/all_gather | solution.py:10
  7.3 103.7 %all-gather.3.cloned.1.call-start = ((), (), s32[]{:S(2)}) async-start(), calls=%async_computation | async-start | bytes 4718592 | tf_op jit(solution)/shard_map/all_gather | solution.py:21
Sparse Core Ops, SparseCore 0:
  8.9 25.2 all-gather.4
  36.2 74.6 all-gather.2
where the time goes:
time: 147 us
  waiting for transfers between devices  104 us (71%)
  blocking collectives  18.6 us (13%)
  between operations  13.4 us (9%)
  matrix products  6.56 us (4%)
  other arithmetic  1.82 us (1%)
  local copies, waits for them, and re-layouts  1.81 us (1%)
    all_gather x1, waiting for transfers between devices, shards(): left_line = lax.all_gather(left_factor, 'east', axis=1, tiled=True)  76.7 us
    all_gather x1, waiting for transfers between devices, gathered(): return lax.all_gather(part, axis, axis=dim, tiled=True)  26.2 us
    psum x1, blocking collectives, shards(): row_power = lax.psum(jnp.sum(updated * updated, axis=1), 'east')  18.6 us
    dot_general x1, matrix products, absorb_panel(): jnp.dot(left_panel, right_panel, preferred_element_type=jnp.float32)  6.56 us
  transfers between devices with their start and end apart: 2, of which 2 were waited for; matrix products, arithmetic and copies ran while one was open for 0% of the time, Pallas kernels for 0%

commit v1 on v0

--- a/solution.py
+++ b/solution.py
@@ -26,7 +26,7 @@
 
     total = over_all(right_factor, "north", 0, take_rows, begin)
     updated = total
-    row_power = lax.psum(jnp.sum(updated * updated, axis=1), "east")
+    row_power = jnp.sum(lax.all_gather(jnp.sum(updated * updated, axis=1), "east"), axis=0)
     updated = (
         updated * lax.rsqrt(row_power / (updated.shape[1] * lax.axis_size("east")) + 1e-06)[:, None]
     )

time: 147 us -> 159 us (1.082)
  blocking collectives: 18.6 us -> 30.6 us
    all_gather x0 -> x1, blocking collectives: none -> 30.6 us  [shards(): lax.all_gather(jnp.sum(updated * updated, axis=1), 'east')]
    psum x1 -> x0, blocking collectives: 18.6 us -> none  [shards(): row_power = lax.psum(jnp.sum(updated * updated, axis=1), 'east')]
where the time goes in v1:
time: 159 us
  waiting for transfers between devices  104 us (65%)
  blocking collectives  30.6 us (19%)
  between operations  13.4 us (8%)
  matrix products  6.56 us (4%)
  local copies, waits for them, and re-layouts  1.83 us (1%)
  other arithmetic  1.83 us (1%)
    all_gather x1, waiting for transfers between devices, shards(): left_line = lax.all_gather(left_factor, 'east', axis=1, tiled=True)  76.7 us
    all_gather x1, blocking collectives, shards(): lax.all_gather(jnp.sum(updated * updated, axis=1), 'east')  30.6 us
    all_gather x1, waiting for transfers between devices, gathered(): return lax.all_gather(part, axis, axis=dim, tiled=True)  26.2 us
    dot_general x1, matrix products, absorb_panel(): jnp.dot(left_panel, right_panel, preferred_element_type=jnp.float32)  6.56 us
  transfers between devices with their start and end apart: 2, of which 2 were waited for; matrix products, arithmetic and copies ran while one was open for 0% of the time, Pallas kernels for 0%

profile of v1, /device:TPU:0, one launch (start us, length us, event | category | flops | bytes accessed | tf_op | source)
XLA Modules:
  0.0 158.6 jit_solution(6514375785777202662)
XLA Ops:
  6.5 0.0 all-gather.6.cloned.1.call-start
  6.5 0.7 all-gather.6.cloned.1.call-update
  7.3 0.0 all-gather.4.cloned.1.call-start
  7.3 0.7 all-gather.4.cloned.1.call-update
  8.0 26.2 %all-gather.6.cloned.1.call-done = bf16[2048,512]{1,0:T(8,128)(2,1)} async-done(((bf16[512,512]{1,0:T(8,128)(2,1)}), bf16[2048,512]{1,0:T(8,128)(2,1)}) %all-gather.6.cloned.1.call-update) | async-done | bytes 2097168 | tf_op jit(solution)/shard_map/all_gather | solution.py:10
  34.2 76.7 %all-gather.4.cloned.1.call-done = bf16[1024,2048]{1,0:T(8,128)(2,1)} async-done(((bf16[1024,256]{1,0:T(8,128)(2,1)}), bf16[1024,2048]{1,0:T(8,128)(2,1)}) %all-gather.4.cloned.1.call-update) | async-done | bytes 4194320 | tf_op jit(solution)/shard_map/all_gather | solution.py:21
  110.9 6.6 %multiply_reduce_fusion = (f32[1024]{0:T(1024)S(1)}, f32[1024,512]{0,1:T(8,128)}) fusion(bf16[1024,2048]{1,0:T(8,128)(2,1)} %all-gather.4.cloned.1.call-done, bf16[2048,512]{1,0:T(8,128)(2,1)} %all-gather.6.cloned.1.call-done), kind=kOutput, calls=%fused_computation | convolution fusion | flops 2148531200 | bytes 8392704 | tf_op jit(solution)/shard_map/dot_general | solution.py:16
  117.5 30.6 %all-gather = f32[8192]{0:T(1024)S(1)} all-gather(f32[1024]{0:T(1024)S(1)} %get-tuple-element.5), channel_id=2, replica_groups=mesh['north'=4,'east'=8] {'east'}, dimensions={0}, use_global_device_ids=true | all-gather | bytes 36864 | tf_op jit(solution)/shard_map/all_gather | solution.py:29
  148.1 1.8 %broadcast_multiply_fusion = f32[1024,512]{0,1:T(8,128)S(1)} fusion(f32[1024,512]{0,1:T(8,128)} %get-tuple-element.6, f32[1024]{0:T(1024)S(1)} %add_rsqrt_fusion), kind=kLoop, calls=%fused_computation.1 | loop fusion | flops 524288 | bytes 4198400 | tf_op jit(solution)/shard_map/mul | solution.py:31
  149.9 1.8 %copy.5 = f32[1024,512]{1,0:T(8,128)} copy(f32[1024,512]{0,1:T(8,128)S(1)} %broadcast_multiply_fusion) | data formatting | bytes 4194304 | tf_op jit(solution)/shard_map/mul | solution.py:31
  (3 shorter events, 0.0 us)
Async XLA Ops:
  6.5 27.7 %all-gather.6.cloned.1.call-start = ((), (), s32[]{:S(2)}) async-start(), calls=%async_computation.1 | async-start | bytes 2621440 | tf_op jit(solution)/shard_map/all_gather | solution.py:10
  7.3 103.7 %all-gather.4.cloned.1.call-start = ((), (), s32[]{:S(2)}) async-start(), calls=%async_computation | async-start | bytes 4718592 | tf_op jit(solution)/shard_map/all_gather | solution.py:21
Sparse Core Ops, SparseCore 0:
  8.9 25.2 all-gather.5
  36.2 74.6 all-gather.3
